TPU v7x, 32 devices: a whole 2x2x4 slice. The times are simulated.
32 devices in a mesh: prow: 4 (over y, core), pcol: 8 (over z, x).
Axes of the slice: x: 2, y: 2, z: 4, core: 2. Of those that a mesh axis runs over, the one named last changes fastest.
Arguments:
- slab: bfloat16 [8192, 3072], P('prow', 'pcol'), may hold values from -6 to 6
- pivots: int32 [512], replicated, may hold values from 0 to 8191, as said below
- l_top: bfloat16 [512, 512], replicated, may hold values from -0.125 to 0.125
- l_panel_t: bfloat16 [512, 8192], P('pcol', 'prow'), may hold values from -0.125 to 0.125
Outputs:
- result: bfloat16 [8192, 3072], P('prow', 'pcol')
Inputs may be any that keep to these rules, and one draw needn't show every extreme that they name: `pivots`: distinct rows; how many fall on each index of prow is uneven and changes with the draw.
All inputs are finite; a program needn't handle non-finite values.
Results may differ from a plain program's by a relative error of at most 0.0029.
Values may be sent and summed in bfloat16 or wider, within the bound.
A program may use at most 64 MiB of HBM per device.

v0:
```python
import functools

import jax
import jax.numpy as jnp
from jax import lax
from jax.experimental import pallas as pl
from jax.experimental.pallas import tpu as pltpu
from jax.sharding import PartitionSpec as P

MESH = pl.DeviceIdType.MESH
F32 = jnp.float32
BF16 = jnp.bfloat16
LANES = 128


def in_turn(first, second):
    first()
    second()


def dot(a, b):
    return jnp.dot(a, b, preferred_element_type=F32)


def dot_high(a, b):
    return jnp.dot(a, b, preferred_element_type=F32, precision=lax.Precision.HIGHEST)


def iota(shape, axis):
    return lax.broadcasted_iota(jnp.int32, shape, axis)


def cuts(width):
    units = width // LANES
    edges = [(units * part) // 16 * LANES for part in (0, 6, 15, 16)]
    return [(a, b - a) for a, b in zip(edges[:-1], edges[1:])]


def kernel(
    n_prow, n_pcol,
    slab_hbm, pivots_ref, l_top_hbm, panel_hbm, out_ref,
    slab_ref, l_top_ref, gathered, picked, picked_in, merged, homes, pivoted, inverse_hi, inverse_lo, high, u_ref,
    local_sem, panel_recv, panel_send, core_sem, chip_send, chip_recv, relay_send, relay_recv,
):
    block = l_top_ref.shape[0]
    rows, width = slab_ref.shape
    me_r = lax.axis_index("prow")
    me_c = lax.axis_index("pcol")
    chips = n_prow // 2
    chip, core = me_r // 2, me_r % 2
    peer = me_r + 1 - 2 * core
    length = n_pcol // 2
    z, x = me_c // 2, me_c % 2
    other = 1 - x
    pieces = cuts(gathered.shape[2])
    bulk = range(len(pieces) - 1)
    rest = len(pieces) - 1

    slab_copy = pltpu.make_async_copy(slab_hbm, slab_ref, local_sem.at[0])
    panel_copy = pltpu.make_async_copy(panel_hbm, gathered.at[me_c], local_sem.at[1])
    panel_copy.start()
    slab_copy.start()
    l_top_copy = pltpu.make_async_copy(l_top_hbm, l_top_ref, local_sem.at[2])
    l_top_copy.start()

    barrier = pltpu.get_barrier_semaphore()

    def greet(r, c):
        pl.semaphore_signal(barrier, inc=1, device_id=(r, c), device_id_type=MESH)

    greet(peer, me_c)
    greet(me_r, z * 2 + other)
    for step in range(1, chips):
        greet(((chip + step) % chips) * 2 + core, me_c)

    @pl.when(z > 0)
    def _():
        greet(me_r, me_c - 2)

    @pl.when(z < length - 1)
    def _():
        greet(me_r, me_c + 2)

    has_below = (z + length - 1) // length
    has_above = (2 * length - 2 - z) // length
    pl.semaphore_wait(barrier, 1 + chips + has_below + has_above)

    panel_copy.wait()

    def send(way, source, piece):
        start, size = pieces[piece]
        target = (me_c + 2, me_c - 2, z * 2 + other)[way]
        part = gathered.at[source, :, pl.ds(start, size)]
        return pltpu.make_async_remote_copy(
            src_ref=part, dst_ref=part,
            send_sem=panel_send.at[way, source, piece],
            recv_sem=panel_recv.at[source, piece],
            device_id=(me_r, target), device_id_type=MESH,
        )

    def along(source, piece, ways=(0, 1)):
        if 0 in ways:
            @pl.when(z < length - 1)
            def _():
                send(0, source, piece).start()
        if 1 in ways:
            @pl.when(z > 0)
            def _():
                send(1, source, piece).start()

    def arrived(source, piece):
        send(2, source, piece).wait_recv()

    def first_sends():
        send(2, me_c, rest).start()
        for piece in bulk:
            along(me_c, piece)
            send(2, me_c, piece).start()

    def relay_bulk(distance, piece):
        below = (z - distance) * 2 + x
        above = (z + distance) * 2 + x

        @pl.when(z >= distance)
        def _():
            arrived(below, piece)

            @pl.when(z < length - 1)
            def _():
                send(0, below, piece).start()
            send(2, below, piece).start()

        @pl.when(z < length - distance)
        def _():
            arrived(above, piece)

            @pl.when(z > 0)
            def _():
                send(1, above, piece).start()
            send(2, above, piece).start()

    def own_rest(distance):
        if distance == 0:
            arrived(z * 2 + other, rest)
        for source in (me_c, z * 2 + other):
            @pl.when((z == distance) & (z < length - 1))
            def _():
                send(0, source, rest).start()

            @pl.when((length - 1 - z == distance) & (z > 0))
            def _():
                send(1, source, rest).start()

    def relay_rest(distance):
        for side in (x, other):
            below = (z - distance) * 2 + side
            above = (z + distance) * 2 + side

            @pl.when(z >= distance)
            def _():
                arrived(below, rest)

                @pl.when(z < length - 1)
                def _():
                    send(0, below, rest).start()

            @pl.when(z < length - distance)
            def _():
                arrived(above, rest)

                @pl.when(z > 0)
                def _():
                    send(1, above, rest).start()

    def each_line(act):
        for at in range(length):
            act(at)

    def last_arrivals():
        for at in range(length):
            for piece in bulk:
                arrived(at * 2 + other, piece)

    def drain():
        for at in range(length):
            for side in (0, 1):
                source = at * 2 + side
                for piece in range(len(pieces)):
                    def up():
                        send(0, source, piece).wait_send()

                    def down():
                        send(1, source, piece).wait_send()

                    use = (piece == rest) | (x == side)
                    pl.when(use & (z < length - 1) & (at <= z))(up)
                    pl.when(use & (z > 0) & (at >= z))(down)
                    if piece == rest:
                        pl.when((x == side) & (at == z))(lambda: send(2, source, piece).wait_send())
                    else:
                        pl.when(x == side)(lambda: send(2, source, piece).wait_send())

    state = {}
    ii = iota((block, block), 0)
    jj = iota((block, block), 1)

    def column(row):
        return jnp.sum(jnp.where(ii == jj, row, 0.0), axis=1, keepdims=True)

    def bookkeeping():
        pivot_row = pivots_ref[...].astype(F32)
        pivot_col = column(pivot_row)
        chosen = jnp.max(jnp.where(pivot_col == jj.astype(F32), 1.0, 0.0), axis=0, keepdims=True)
        free = 1.0 - chosen
        far = jnp.where(pivot_row >= block, 1.0, 0.0)
        which = iota((16, block), 0)
        both = jnp.where(which == 0, free, jnp.where(which == 1, far, 0.0))
        ranks = dot(both.astype(BF16), jnp.where(ii < jj, 1.0, 0.0).astype(BF16))
        far_rank = column(ranks[1:2])
        match = (free > 0.5) & (ranks[0:1] == far_rank)
        source = jnp.sum(jnp.where(match, jj.astype(F32), 0.0), axis=1, keepdims=True)
        state.update(pivot_row=pivot_row, pivot_col=pivot_col, source=source)

    def pick():
        pivot_col, source = state["pivot_col"], state["source"]
        first = (me_r * rows).astype(F32)
        mine = (pivot_col >= first) & (pivot_col < first + rows)
        lead = (me_r == 0).astype(F32)
        index = jnp.where(mine, pivot_col - first, source * lead - (1.0 - lead))
        slab_copy.wait()
        total = jnp.zeros((block, width), F32)
        for start in range(0, rows, block):
            hot = jnp.where((jj + start).astype(F32) == index, 1.0, 0.0).astype(BF16)
            total = total + dot(hot, slab_ref[start:start + block, :])
        picked[...] = total.astype(BF16)

    def core_copy():
        return pltpu.make_async_remote_copy(
            src_ref=picked, dst_ref=picked_in, send_sem=core_sem.at[0], recv_sem=core_sem.at[1],
            device_id=(peer, me_c), device_id_type=MESH,
        )

    def own_homes():
        homes[:, width:] = jnp.ones((block, LANES), BF16)

        @pl.when(me_r == 0)
        def _():
            hot = jnp.where(jj.astype(F32) == state["source"], 1.0, 0.0).astype(BF16)
            homes[:, :width] = dot(hot, slab_ref[:block, :]).astype(BF16)

    half = block // 2

    def chip_copy(step):
        rows_of = pl.ds(pl.multiple_of(core * half, half), half)
        to = ((chip + step) % chips) * 2 + core
        return pltpu.make_async_remote_copy(
            src_ref=merged.at[0, rows_of], dst_ref=merged.at[step, rows_of],
            send_sem=chip_send.at[step], recv_sem=chip_recv.at[step],
            device_id=(to, me_c), device_id_type=MESH,
        )

    def relay_copy(step):
        part = merged.at[step, pl.ds(pl.multiple_of(core * half, half), half)]
        return pltpu.make_async_remote_copy(
            src_ref=part, dst_ref=part, send_sem=relay_send.at[step], recv_sem=relay_recv.at[step],
            device_id=(peer, me_c), device_id_type=MESH,
        )

    def merge():
        core_copy().wait()
        pivot_col = state["pivot_col"]
        lead = (chip == 0).astype(F32)
        second = jnp.where((pivot_col >= rows) & (pivot_col < 2 * rows), lead, 0.0)
        mine, theirs = picked[...].astype(F32), picked_in[...].astype(F32)
        even = (core == 0).astype(F32)
        keep_mine = 1.0 - even * second
        keep_theirs = 1.0 - (1.0 - even) * second
        merged[0] = (mine * keep_mine + theirs * keep_theirs).astype(BF16)
        for step in range(1, chips):
            chip_copy(step).start()

    def relay_chips():
        for step in range(1, chips):
            chip_copy(step).wait()
            relay_copy(step).start()

    def assemble():
        for step in range(1, chips):
            relay_copy(step).wait()
        pivot_col = state["pivot_col"]
        top = jnp.zeros((block, width), F32)
        for step in range(chips):
            low = (((chip + chips - step) % chips) * 2 * rows).astype(F32)
            here = (pivot_col >= low) & (pivot_col < low + 2 * rows)
            top = top + jnp.where(here, merged[step].astype(F32), 0.0)
        state["top"] = top.astype(BF16)

        @pl.when(me_r == 1)
        def _():
            homes[:, :width] = picked_in[...]

        for step in range(1, chips):
            @pl.when((chip > 0) & (chip == step))
            def _():
                homes[:, :width] = merged[step]

    def interchange(start):
        def act():
            row = iota((block, block), 0) + (me_r * rows + start)
            pivot_row = state["pivot_row"]
            hot = jnp.where((row.astype(F32) == pivot_row) & (pivot_row >= block), 1.0, 0.0)
            both = dot(hot.astype(BF16), homes[...])
            taken = both[:, width:] > 0.5
            for lane in range(0, width, LANES):
                kept = slab_ref[start:start + block, lane:lane + LANES].astype(F32)
                new = jnp.where(taken, both[:, lane:lane + LANES], kept)
                pivoted[start:start + block, lane:lane + LANES] = new.astype(BF16)
        return act

    base = min(block, 256)
    small = min(base, 16)
    bi = iota((base, base), 0)
    bj = iota((base, base), 1)
    groups = block // base

    def diagonal(g):
        part = l_top_ref[g * base:(g + 1) * base, g * base:(g + 1) * base].astype(F32)
        return jnp.where(bi > bj, part, 0.0)

    def start_inverse():
        l_top_copy.wait()
        state["x"], state["power"] = [], []
        for g in range(groups):
            near = jnp.where(bi // small == bj // small, diagonal(g), 0.0)
            state["x"].append(jnp.where(bi == bj, 1.0, 0.0) - near)
            state["power"].append(near)

    def power_step():
        for g in range(groups):
            square = dot_high(state["power"][g], state["power"][g])
            state["power"][g] = square
            state["x"][g] = state["x"][g] + dot_high(state["x"][g], square)

    def double(size):
        def act():
            for g in range(groups):
                link = jnp.where(
                    (bi // (2 * size) == bj // (2 * size)) & (bi // size != bj // size), diagonal(g), 0.0
                )
                inv = state["x"][g]
                state["x"][g] = inv - dot_high(inv, dot_high(link, inv))
        return act

    def join():
        for g in range(groups):
            high[g * base:(g + 1) * base, :] = jnp.zeros((base, block), F32)
            high[g * base:(g + 1) * base, g * base:(g + 1) * base] = state["x"][g]

    def join_double(size):
        def act():
            for at in range(0, block, 2 * size):
                a = high[at:at + size, at:at + size]
                b = high[at + size:at + 2 * size, at + size:at + 2 * size]
                c = l_top_ref[at + size:at + 2 * size, at:at + size].astype(F32)
                high[at + size:at + 2 * size, at:at + size] = -dot_high(b, dot_high(c, a))
        return act

    def split():
        whole = high[...]
        top_bits = whole.astype(BF16)
        inverse_hi[...] = top_bits
        inverse_lo[...] = (whole - top_bits.astype(F32)).astype(BF16)

    def solve():
        top = state["top"]
        u_ref[...] = (dot(inverse_hi[...], top) + dot(inverse_lo[...], top)).astype(BF16)

    inverse = [start_inverse]
    size = 2
    while size < small:
        inverse.append(power_step)
        size *= 2
    size = small
    while size < base:
        inverse.append(double(size))
        size *= 2
    inverse.append(join)
    while size < block:
        inverse.append(join_double(size))
        size *= 2
    inverse.append(split)

    first_sends()
    bookkeeping()
    pick()
    core_copy().start()
    own_homes()
    events = [functools.partial(own_rest, 0)]
    for distance in range(1, length):
        events += [functools.partial(relay_bulk, distance, piece) for piece in bulk]
        events[-1] = functools.partial(in_turn, events[-1], functools.partial(own_rest, distance))
    events += [functools.partial(relay_rest, distance) for distance in range(1, length)]
    work = [inverse[0], merge] + inverse[1:7] + [relay_chips] + inverse[7:] + [assemble, solve]
    work += [interchange(start) for start in range(0, rows, block)]
    events.append(last_arrivals)
    per = -(-len(work) // max(1, len(events) - 1))
    for event in events[:-1]:
        event()
        for act in work[:per]:
            act()
        work = work[per:]
    for act in work:
        act()
    events[-1]()

    for start in range(0, rows, block):
        panel = gathered[:, :, start:start + block].reshape(block, block).astype(BF16)
        product = lax.dot_general(
            panel, u_ref[...], (((0,), (0,)), ((), ())), preferred_element_type=F32
        )
        out_ref[start:start + block, :] = (pivoted[start:start + block, :].astype(F32) - product).astype(BF16)

    @pl.when(me_r == 0)
    def _():
        out_ref[:block, :] = u_ref[...]

    drain()


def per_device(n_prow, n_pcol, slab, pivots, l_top, l_panel_t):
    rows, width = slab.shape
    block = pivots.shape[0]
    depth = l_panel_t.shape[0]
    kind = BF16 if depth % 16 == 0 else F32
    panel = l_panel_t.astype(kind)
    chips = n_prow // 2
    n_pieces = len(cuts(rows))
    vmem = pl.BlockSpec(memory_space=pltpu.VMEM)
    anywhere = pl.BlockSpec(memory_space=pltpu.HBM)
    dma = pltpu.SemaphoreType.DMA
    return pl.pallas_call(
        functools.partial(kernel, n_prow, n_pcol),
        out_shape=pltpu.VMEM((rows, width), BF16),
        in_specs=[anywhere, vmem, anywhere, anywhere],
        out_specs=vmem,
        scratch_shapes=[
            pltpu.VMEM((rows, width), BF16),
            pltpu.VMEM((block, block), BF16),
            pltpu.VMEM((n_pcol, depth, rows), kind),
            pltpu.VMEM((block, width), BF16),
            pltpu.VMEM((block, width), BF16),
            pltpu.VMEM((chips, block, width), BF16),
            pltpu.VMEM((block, width + LANES), BF16),
            pltpu.VMEM((rows, width), BF16),
            pltpu.VMEM((block, block), BF16),
            pltpu.VMEM((block, block), BF16),
            pltpu.VMEM((block, block), F32),
            pltpu.VMEM((block, width), BF16),
            dma((3,)),
            dma((n_pcol, n_pieces)),
            dma((3, n_pcol, n_pieces)),
            dma((2,)),
            dma((chips,)),
            dma((chips,)),
            dma((chips,)),
            dma((chips,)),
        ],
        compiler_params=pltpu.CompilerParams(collective_id=0, has_side_effects=True, vmem_limit_bytes=60 * 2**20),
    )(slab, pivots.reshape(1, block), l_top, panel)


def solution(mesh):
    return jax.shard_map(
        functools.partial(per_device, mesh.shape["prow"], mesh.shape["pcol"]),
        mesh=mesh,
        in_specs=(P("prow", "pcol"), P(), P(), P("pcol", "prow")),
        out_specs=P("prow", "pcol"),
        check_vma=False,
    )
```

profile of v0, /device:TPU:0, one launch (start us, length us, event | category | flops | bytes accessed | tf_op | source)
XLA Modules:
  0.0 30.9 jit_solution(13515391228155160597)
XLA Ops:
  0.0 29.7 %shard_map.46 = bf16[2048,384]{1,0:T(8,128)(2,1)S(1)} custom-call(bf16[2048,384]{1,0:T(8,128)(2,1)} %slab_hbm.1, s32[1,512]{1,0:T(1,128)} %bitcast.1, bf16[512,512]{1,0:T(8,128)(2,1)} %l_top_hbm.1, bf16[64,2048]{1,0:T(8,128)(2,1)} %panel_hbm.1), custom_call_target="tpu_custom_call" | custom-call | tf_op jit(solution)/shard_map/pallas_call | solution.py:441
  29.7 1.1 %copy.6 = bf16[2048,384]{1,0:T(8,128)(2,1)} copy(bf16[2048,384]{1,0:T(8,128)(2,1)S(1)} %shard_map.46) | data formatting | bytes 3145728
where the time goes:
time: 31.1 us; the launch traced here: 30.9 us
  Pallas kernels  29.7 us (95%)
  local copies, waits for them, and re-layouts  1.15 us (4%)
    pallas_call x1, Pallas kernels, per_device(): pl.pallas_call(functools.partial(kernel, n_prow, n_pcol), out_shape=pltpu...  29.7 us
    unnamed x1, local copies, waits for them, and re-layouts  1.15 us

commit v1 on v0

v1 whole, which is shorter than its diff:
```python
import functools

import jax
import jax.numpy as jnp
from jax import lax
from jax.experimental import pallas as pl
from jax.experimental.pallas import tpu as pltpu
from jax.sharding import PartitionSpec as P

MESH = pl.DeviceIdType.MESH
F32 = jnp.float32
BF16 = jnp.bfloat16
LANES = 128


def dot(a, b):
    return jnp.dot(a, b, preferred_element_type=F32)


def iota(shape, axis):
    return lax.broadcasted_iota(jnp.int32, shape, axis)


def halves(a):
    high = a.astype(BF16)
    return high, (a - high.astype(F32)).astype(BF16)


def dot_exact_left(a, b):
    high, low = halves(b)
    return dot(a, high) + dot(a, low)


def dot_split(a, b):
    a_high, a_low = halves(a)
    b_high, b_low = halves(b)
    return dot(a_high, b_high) + (dot(a_high, b_low) + dot(a_low, b_high))


EDGES = (0, 2, 6, 10, 13, 16)


def cuts(width):
    units = width // LANES
    edges = [(units * part) // 16 * LANES for part in EDGES]
    return [(a, b - a) for a, b in zip(edges[:-1], edges[1:])]


def weave(events, work):
    plan, count = [], max(1, len(events))
    for at, event in enumerate(events):
        plan += [event] + work[at * len(work) // count:(at + 1) * len(work) // count]
    return plan


def kernel(
    n_prow, n_pcol,
    slab_hbm, pivots_hbm, l_top_hbm, panel_hbm, out_ref,
    slab_ref, pivots_ref, l_top_ref, gathered, picked, picked_in, merged, homes, pivoted, inverse_hi, inverse_lo, high,
    u_ref,
    local_sem, line_recv, cross_recv, rest_recv, sent, core_sem, chip_send, chip_recv, relay_send, relay_recv,
):
    block = l_top_ref.shape[0]
    rows, width = slab_ref.shape
    me_r = lax.axis_index("prow")
    me_c = lax.axis_index("pcol")
    chips = n_prow // 2
    chip, core = me_r // 2, me_r % 2
    peer = me_r + 1 - 2 * core
    length = n_pcol // 2
    z, x = me_c // 2, me_c % 2
    other = 1 - x
    pieces = cuts(gathered.shape[2])
    bulk = range(len(pieces) - 1)
    rest = len(pieces) - 1

    panel_copy = pltpu.make_async_copy(panel_hbm, gathered.at[me_c], local_sem.at[0])
    pivots_copy = pltpu.make_async_copy(pivots_hbm, pivots_ref, local_sem.at[1])
    slab_copy = pltpu.make_async_copy(slab_hbm, slab_ref, local_sem.at[2])
    l_top_copy = pltpu.make_async_copy(l_top_hbm, l_top_ref, local_sem.at[3])

    barrier = pltpu.get_barrier_semaphore()

    def greet(r, c):
        pl.semaphore_signal(barrier, inc=1, device_id=(r, c), device_id_type=MESH)

    greet(me_r, z * 2 + other)

    @pl.when(z > 0)
    def _():
        greet(me_r, me_c - 2)

    @pl.when(z < length - 1)
    def _():
        greet(me_r, me_c + 2)

    for step in range(1, chips):
        greet(((chip + step) % chips) * 2 + core, me_c)
    greet(peer, me_c)

    panel_copy.start()
    pivots_copy.start()
    slab_copy.start()
    l_top_copy.start()

    has_below = (z + length - 1) // length
    has_above = (2 * length - 2 - z) // length

    def strip(source, piece):
        start, size = pieces[piece]
        return gathered.at[source, :, pl.ds(start, size)]

    def send(part, send_sem, recv_sem, target):
        return pltpu.make_async_remote_copy(
            src_ref=part, dst_ref=part, send_sem=send_sem, recv_sem=recv_sem,
            device_id=(me_r, target), device_id_type=MESH,
        )

    def line(way, at, piece):
        target = me_c + 2 - 4 * way
        return send(strip(at * 2 + x, piece), sent.at[way], line_recv.at[at, piece], target)

    def line_rest(way, at, side):
        target = me_c + 2 - 4 * way
        return send(strip(at * 2 + side, rest), sent.at[2 + way], rest_recv.at[at, side], target)

    def cross(at, piece):
        return send(strip(at * 2 + x, piece), sent.at[4], cross_recv.at[piece], z * 2 + other)

    def cross_rest():
        return send(strip(me_c, rest), sent.at[5], rest_recv.at[z, x], z * 2 + other)

    def both_ways(start):
        pl.when(z < length - 1)(lambda: start(0))
        pl.when(z > 0)(lambda: start(1))

    def first_sends():
        for piece in bulk:
            both_ways(lambda way: line(way, z, piece).start())
            cross(z, piece).start()
            if piece == min(1, rest - 1):
                cross_rest().start()

    def send_rest():
        both_ways(lambda way: line_rest(way, z, x).start())

    def own_rest():
        send(strip(z * 2 + other, rest), sent.at[5], rest_recv.at[z, other], z * 2 + other).wait_recv()
        both_ways(lambda way: line_rest(way, z, other).start())

    def relay(distance, piece):
        def act():
            for way, at, reached, onward in (
                (0, z - distance, z >= distance, z < length - 1),
                (1, z + distance, z < length - distance, z > 0),
            ):
                @pl.when(reached)
                def _():
                    line(way, at, piece).wait_recv()
                    pl.when(onward)(lambda: line(way, at, piece).start())
                    cross(at, piece).start()
        return act

    def relay_rest(distance):
        def act():
            for way, at, reached in (
                (0, z - distance, (z >= distance) & (z < length - 1)),
                (1, z + distance, (z < length - distance) & (z > 0)),
            ):
                @pl.when(reached)
                def _():
                    for side in (0, 1):
                        line_rest(way, at, side).wait_recv()
                        line_rest(way, at, side).start()
        return act

    def last_rests():
        for distance in range(1, length):
            for way, at, reached in (
                (0, z - distance, (z >= distance) & (z == length - 1)),
                (1, z + distance, (z < length - distance) & (z == 0)),
            ):
                @pl.when(reached)
                def _():
                    for side in (0, 1):
                        line_rest(way, at, side).wait_recv()

    def crossed(piece):
        start, size = pieces[piece]
        every = gathered.at[pl.ds(0, length), :, pl.ds(start, size)]
        send(every, sent.at[4], cross_recv.at[piece], z * 2 + other).wait_recv()

    def drain():
        wide = sum(pieces[piece][1] for piece in bulk)
        thin = pieces[rest][1]

        def gone(sem, count, size):
            part = gathered.at[pl.ds(0, count), :, pl.ds(0, size)]
            send(part, sent.at[sem], rest_recv.at[0, 0], z * 2 + other).wait_send()

        def gone_line(way, count):
            gone(way, count, wide)
            gone(2 + way, count, 2 * thin)

        for at in range(length):
            if at < length - 1:
                pl.when(z == at)(lambda: gone_line(0, at + 1))
            if at > 0:
                pl.when(z == at)(lambda: gone_line(1, length - at))
        gone(4, length, wide)
        gone(5, 1, thin)

    state = {}
    ii = iota((block, block), 0)
    jj = iota((block, block), 1)

    def column(row):
        return jnp.sum(jnp.where(ii == jj, row, 0.0), axis=1, keepdims=True)

    def bookkeeping():
        pivots_copy.wait()
        pivot_row = pivots_ref[...].astype(F32)
        pivot_col = column(pivot_row)
        chosen = jnp.max(jnp.where(pivot_col == jj.astype(F32), 1.0, 0.0), axis=0, keepdims=True)
        free = 1.0 - chosen
        far = jnp.where(pivot_row >= block, 1.0, 0.0)
        which = iota((16, block), 0)
        both = jnp.where(which == 0, free, jnp.where(which == 1, far, 0.0))
        ranks = dot(both.astype(BF16), jnp.where(ii < jj, 1.0, 0.0).astype(BF16))
        far_rank = column(ranks[1:2])
        match = (free > 0.5) & (ranks[0:1] == far_rank)
        source = jnp.sum(jnp.where(match, jj.astype(F32), 0.0), axis=1, keepdims=True)
        state.update(pivot_row=pivot_row, pivot_col=pivot_col, source=source)

    def pick():
        pivot_col, source = state["pivot_col"], state["source"]
        first = (me_r * rows).astype(F32)
        mine = (pivot_col >= first) & (pivot_col < first + rows)
        lead = (me_r == 0).astype(F32)
        index = jnp.where(mine, pivot_col - first, source * lead - (1.0 - lead))
        slab_copy.wait()
        total = jnp.zeros((block, width), F32)
        for start in range(0, rows, block):
            hot = jnp.where((jj + start).astype(F32) == index, 1.0, 0.0).astype(BF16)
            total = total + dot(hot, slab_ref[start:start + block, :])
        picked[...] = total.astype(BF16)

    def core_copy():
        return pltpu.make_async_remote_copy(
            src_ref=picked, dst_ref=picked_in, send_sem=core_sem.at[0], recv_sem=core_sem.at[1],
            device_id=(peer, me_c), device_id_type=MESH,
        )

    def own_homes():
        homes[:, width:] = jnp.ones((block, LANES), BF16)

        @pl.when(me_r == 0)
        def _():
            hot = jnp.where(jj.astype(F32) == state["source"], 1.0, 0.0).astype(BF16)
            homes[:, :width] = dot(hot, slab_ref[:block, :]).astype(BF16)

    half = block // 2

    def chip_copy(step):
        rows_of = pl.ds(pl.multiple_of(core * half, half), half)
        to = ((chip + step) % chips) * 2 + core
        return pltpu.make_async_remote_copy(
            src_ref=merged.at[0, rows_of], dst_ref=merged.at[step, rows_of],
            send_sem=chip_send.at[step - 1], recv_sem=chip_recv.at[step - 1],
            device_id=(to, me_c), device_id_type=MESH,
        )

    def relay_copy(step):
        part = merged.at[step, pl.ds(pl.multiple_of(core * half, half), half)]
        return pltpu.make_async_remote_copy(
            src_ref=part, dst_ref=part, send_sem=relay_send.at[step - 1], recv_sem=relay_recv.at[step - 1],
            device_id=(peer, me_c), device_id_type=MESH,
        )

    def merge():
        core_copy().wait()
        pivot_col = state["pivot_col"]
        lead = (chip == 0).astype(F32)
        second = jnp.where((pivot_col >= rows) & (pivot_col < 2 * rows), lead, 0.0)
        mine, theirs = picked[...].astype(F32), picked_in[...].astype(F32)
        even = (core == 0).astype(F32)
        keep_mine = 1.0 - even * second
        keep_theirs = 1.0 - (1.0 - even) * second
        merged[0] = (mine * keep_mine + theirs * keep_theirs).astype(BF16)
        for step in range(1, chips):
            chip_copy(step).start()

    def relay_chips():
        for step in range(1, chips):
            chip_copy(step).wait()
            relay_copy(step).start()

    def assemble():
        for step in range(1, chips):
            relay_copy(step).wait()
        pivot_col = state["pivot_col"]
        top = jnp.zeros((block, width), F32)
        for step in range(chips):
            low = (((chip + chips - step) % chips) * 2 * rows).astype(F32)
            here = (pivot_col >= low) & (pivot_col < low + 2 * rows)
            top = top + jnp.where(here, merged[step].astype(F32), 0.0)
        state["top"] = top.astype(BF16)

        @pl.when(me_r == 1)
        def _():
            homes[:, :width] = picked_in[...]

        for step in range(1, chips):
            @pl.when((chip > 0) & (chip == step))
            def _():
                homes[:, :width] = merged[step]

    def interchange(start):
        def act():
            row = iota((block, block), 0) + (me_r * rows + start)
            pivot_row = state["pivot_row"]
            hot = jnp.where((row.astype(F32) == pivot_row) & (pivot_row >= block), 1.0, 0.0)
            both = dot(hot.astype(BF16), homes[...])
            taken = both[:, width:] > 0.5
            for lane in range(0, width, LANES):
                kept = slab_ref[start:start + block, lane:lane + LANES].astype(F32)
                new = jnp.where(taken, both[:, lane:lane + LANES], kept)
                pivoted[start:start + block, lane:lane + LANES] = new.astype(BF16)
        return act

    base = min(block, 256)
    small = min(base, 16)
    bi = iota((base, base), 0)
    bj = iota((base, base), 1)
    groups = block // base

    def diagonal(g):
        part = l_top_ref[g * base:(g + 1) * base, g * base:(g + 1) * base].astype(F32)
        return jnp.where(bi > bj, part, 0.0)

    def start_inverse():
        l_top_copy.wait()
        state["x"], state["power"] = [], []
        for g in range(groups):
            near = jnp.where(bi // small == bj // small, diagonal(g), 0.0)
            state["x"].append(jnp.where(bi == bj, 1.0, 0.0) - near)
            exact = near.astype(BF16)
            state["power"].append(dot(exact, exact))

    def power_step():
        for g in range(groups):
            x, power = state["x"][g], state["power"][g]
            state["x"][g] = x + dot_split(x, power)
            state["power"][g] = dot_split(power, power)

    def last_power():
        for g in range(groups):
            x, power = state["x"][g], state["power"][g]
            state["x"][g] = x + dot_split(x, power)

    def double(size):
        def act():
            for g in range(groups):
                link = jnp.where(
                    (bi // (2 * size) == bj // (2 * size)) & (bi // size != bj // size), diagonal(g), 0.0
                )
                inv = state["x"][g]
                state["x"][g] = inv - dot_split(inv, dot_exact_left(link.astype(BF16), inv))
        return act

    def join():
        for g in range(groups):
            high[g * base:(g + 1) * base, :] = jnp.zeros((base, block), F32)
            high[g * base:(g + 1) * base, g * base:(g + 1) * base] = state["x"][g]

    def join_double(size):
        def act():
            for at in range(0, block, 2 * size):
                a = high[at:at + size, at:at + size]
                b = high[at + size:at + 2 * size, at + size:at + 2 * size]
                c = l_top_ref[at + size:at + 2 * size, at:at + size]
                high[at + size:at + 2 * size, at:at + size] = -dot_split(b, dot_exact_left(c, a))
        return act

    def split():
        inverse_hi[...], inverse_lo[...] = halves(high[...])

    def solve():
        top = state["top"]
        u_ref[...] = (dot(inverse_hi[...], top) + dot(inverse_lo[...], top)).astype(BF16)

    inverse = [start_inverse]
    size = 4
    while size < small:
        inverse.append(power_step)
        size *= 2
    if small > 2:
        inverse.append(last_power)
    size = small
    while size < base:
        inverse.append(double(size))
        size *= 2
    inverse.append(join)
    while size < block:
        inverse.append(join_double(size))
        size *= 2
    inverse.append(split)

    def update(piece):
        start, size = pieces[piece]
        panel = gathered[:, :, start:start + size].reshape(block, size).astype(BF16)
        product = lax.dot_general(
            panel, u_ref[...], (((0,), (0,)), ((), ())), preferred_element_type=F32
        )
        out_ref[start:start + size, :] = (pivoted[start:start + size, :].astype(F32) - product).astype(BF16)

    pl.semaphore_wait(barrier, 1 + chips + has_below + has_above)
    panel_copy.wait()
    pl.when(core == 0)(first_sends)
    bookkeeping()
    pick()
    core_copy().start()
    pl.when(core == 1)(first_sends)
    own_homes()

    def relays(distance):
        return [relay(distance, piece) for piece in bulk] if distance < length else []

    changes = [interchange(start) for start in range(0, rows, block)]
    plan = inverse[:3] + [merge] + weave(relays(1), [send_rest] + inverse[3:6]) + [own_rest] + inverse[6:8]
    plan += weave(relays(2), inverse[8:10] + [relay_chips] + inverse[10:]) + [relay_rest(1), assemble, solve]
    plan += weave(relays(3), changes[:3] + [relay_rest(2)]) + changes[3:]
    for distance in range(4, length):
        plan += relays(distance) + [relay_rest(distance - 1)]
    plan += [relay_rest(length - 1)]
    for act in plan:
        act()

    for piece in bulk:
        crossed(piece)
        update(piece)
    last_rests()
    update(rest)

    @pl.when(me_r == 0)
    def _():
        out_ref[:block, :] = u_ref[...]

    drain()


def per_device(n_prow, n_pcol, slab, pivots, l_top, l_panel_t):
    rows, width = slab.shape
    block = pivots.shape[0]
    depth = l_panel_t.shape[0]
    kind = BF16 if depth % 16 == 0 else F32
    panel = l_panel_t.astype(kind)
    chips = n_prow // 2
    n_pieces = len(cuts(rows))
    vmem = pl.BlockSpec(memory_space=pltpu.VMEM)
    anywhere = pl.BlockSpec(memory_space=pltpu.HBM)
    dma = pltpu.SemaphoreType.DMA
    return pl.pallas_call(
        functools.partial(kernel, n_prow, n_pcol),
        out_shape=pltpu.VMEM((rows, width), BF16),
        in_specs=[anywhere] * 4,
        out_specs=vmem,
        scratch_shapes=[
            pltpu.VMEM((rows, width), BF16),
            pltpu.VMEM((1, block), jnp.int32),
            pltpu.VMEM((block, block), BF16),
            pltpu.VMEM((n_pcol, depth, rows), kind),
            pltpu.VMEM((block, width), BF16),
            pltpu.VMEM((block, width), BF16),
            pltpu.VMEM((chips, block, width), BF16),
            pltpu.VMEM((block, width + LANES), BF16),
            pltpu.VMEM((rows, width), BF16),
            pltpu.VMEM((block, block), BF16),
            pltpu.VMEM((block, block), BF16),
            pltpu.VMEM((block, block), F32),
            pltpu.VMEM((block, width), BF16),
            dma((4,)),
            dma((n_pcol // 2, n_pieces - 1)),
            dma((n_pieces - 1,)),
            dma((n_pcol // 2, 2)),
            dma((6,)),
            dma((2,)),
            dma((chips - 1,)),
            dma((chips - 1,)),
            dma((chips - 1,)),
            dma((chips - 1,)),
        ],
        compiler_params=pltpu.CompilerParams(collective_id=0, has_side_effects=True, vmem_limit_bytes=60 * 2**20),
    )(slab, pivots.reshape(1, block), l_top, panel)


def solution(mesh):
    return jax.shard_map(
        functools.partial(per_device, mesh.shape["prow"], mesh.shape["pcol"]),
        mesh=mesh,
        in_specs=(P("prow", "pcol"), P(), P(), P("pcol", "prow")),
        out_specs=P("prow", "pcol"),
        check_vma=False,
    )
```

time: 31.1 us -> 28 us (0.900)
  Pallas kernels: 29.7 us -> 26.6 us
    pallas_call x1, Pallas kernels: 29.7 us -> 26.6 us  [per_device(): pl.pallas_call(functools.partial(kernel, n_prow, n_pcol), out_shape=pltpu...]
where the time goes in v1:
time: 28 us; the launch traced here: 27.7 us
  Pallas kernels  26.6 us (95%)
  local copies, waits for them, and re-layouts  1.15 us (4%)
    pallas_call x1, Pallas kernels, per_device(): pl.pallas_call(functools.partial(kernel, n_prow, n_pcol), out_shape=pltpu...  26.6 us
    unnamed x1, local copies, waits for them, and re-layouts  1.15 us

profile of v1, /device:TPU:0, one launch (start us, length us, event | category | flops | bytes accessed | tf_op | source)
XLA Modules:
  0.0 27.7 jit_solution(5449611464514068899)
XLA Ops:
  0.0 26.6 %shard_map.46 = bf16[2048,384]{1,0:T(8,128)(2,1)S(1)} custom-call(bf16[2048,384]{1,0:T(8,128)(2,1)} %slab_hbm.1, s32[1,512]{1,0:T(1,128)} %bitcast.1, bf16[512,512]{1,0:T(8,128)(2,1)} %l_top_hbm.1, bf16[64,2048]{1,0:T(8,128)(2,1)} %panel_hbm.1), custom_call_target="tpu_custom_call" | custom-call | tf_op jit(solution)/shard_map/pallas_call | solution.py:463
  26.6 1.1 %copy.6 = bf16[2048,384]{1,0:T(8,128)(2,1)} copy(bf16[2048,384]{1,0:T(8,128)(2,1)S(1)} %shard_map.46) | data formatting | bytes 3145728

commit v2 on v1

--- a/solution.py
+++ b/solution.py
@@ -37,7 +37,7 @@
     return dot(a_high, b_high) + (dot(a_high, b_low) + dot(a_low, b_high))
 
 
-EDGES = (0, 2, 6, 10, 13, 16)
+EDGES = (0, 4, 8, 11, 13, 16)
 
 
 def cuts(width):
@@ -73,6 +73,14 @@
     pieces = cuts(gathered.shape[2])
     bulk = range(len(pieces) - 1)
     rest = len(pieces) - 1
+    lead = me_r == 0
+
+    def needed(piece, act):
+        start, size = pieces[piece]
+        if start + size <= block:
+            pl.when(jnp.logical_not(lead))(act)
+        else:
+            act()
 
     panel_copy = pltpu.make_async_copy(panel_hbm, gathered.at[me_c], local_sem.at[0])
     pivots_copy = pltpu.make_async_copy(pivots_hbm, pivots_ref, local_sem.at[1])
@@ -136,20 +144,35 @@
 
     def first_sends():
         for piece in bulk:
-            both_ways(lambda way: line(way, z, piece).start())
-            cross(z, piece).start()
-            if piece == min(1, rest - 1):
+            def own():
+                both_ways(lambda way: line(way, z, piece).start())
+                cross(z, piece).start()
+            needed(piece, own)
+            if piece == rest // 2:
                 cross_rest().start()
-
-    def send_rest():
-        both_ways(lambda way: line_rest(way, z, x).start())
-
-    def own_rest():
+        own_rest(0, x)()
+
+    def rest_ways(distance, act):
+        if distance < length - 1:
+            pl.when(z == distance)(lambda: act(0))
+            pl.when(z == length - 1 - distance)(lambda: act(1))
+
+    def own_rest(distance, side):
+        return lambda: rest_ways(distance, lambda way: line_rest(way, z, side).start())
+
+    def other_rest():
         send(strip(z * 2 + other, rest), sent.at[5], rest_recv.at[z, other], z * 2 + other).wait_recv()
-        both_ways(lambda way: line_rest(way, z, other).start())
+
+    def pass_rest(distance, reach):
+        def onward(way):
+            at = z + (2 * way - 1) * reach
+            for side in (0, 1):
+                line_rest(way, at, side).wait_recv()
+                line_rest(way, at, side).start()
+        return lambda: rest_ways(distance, onward)
 
     def relay(distance, piece):
-        def act():
+        def both():
             for way, at, reached, onward in (
                 (0, z - distance, z >= distance, z < length - 1),
                 (1, z + distance, z < length - distance, z > 0),
@@ -159,20 +182,7 @@
                     line(way, at, piece).wait_recv()
                     pl.when(onward)(lambda: line(way, at, piece).start())
                     cross(at, piece).start()
-        return act
-
-    def relay_rest(distance):
-        def act():
-            for way, at, reached in (
-                (0, z - distance, (z >= distance) & (z < length - 1)),
-                (1, z + distance, (z < length - distance) & (z > 0)),
-            ):
-                @pl.when(reached)
-                def _():
-                    for side in (0, 1):
-                        line_rest(way, at, side).wait_recv()
-                        line_rest(way, at, side).start()
-        return act
+        return lambda: needed(piece, both)
 
     def last_rests():
         for distance in range(1, length):
@@ -188,18 +198,24 @@
     def crossed(piece):
         start, size = pieces[piece]
         every = gathered.at[pl.ds(0, length), :, pl.ds(start, size)]
-        send(every, sent.at[4], cross_recv.at[piece], z * 2 + other).wait_recv()
+        needed(piece, lambda: send(every, sent.at[4], cross_recv.at[piece], z * 2 + other).wait_recv())
 
     def drain():
-        wide = sum(pieces[piece][1] for piece in bulk)
         thin = pieces[rest][1]
 
         def gone(sem, count, size):
             part = gathered.at[pl.ds(0, count), :, pl.ds(0, size)]
             send(part, sent.at[sem], rest_recv.at[0, 0], z * 2 + other).wait_send()
 
+        def gone_bulk(sem, count):
+            def wide(first):
+                return sum(size for start, size in pieces[:-1] if start + size > first)
+
+            pl.when(lead)(lambda: gone(sem, count, wide(block)))
+            pl.when(jnp.logical_not(lead))(lambda: gone(sem, count, wide(0)))
+
         def gone_line(way, count):
-            gone(way, count, wide)
+            gone_bulk(way, count)
             gone(2 + way, count, 2 * thin)
 
         for at in range(length):
@@ -207,7 +223,7 @@
                 pl.when(z == at)(lambda: gone_line(0, at + 1))
             if at > 0:
                 pl.when(z == at)(lambda: gone_line(1, length - at))
-        gone(4, length, wide)
+        gone_bulk(4, length)
         gone(5, 1, thin)
 
     state = {}
@@ -236,8 +252,8 @@
         pivot_col, source = state["pivot_col"], state["source"]
         first = (me_r * rows).astype(F32)
         mine = (pivot_col >= first) & (pivot_col < first + rows)
-        lead = (me_r == 0).astype(F32)
-        index = jnp.where(mine, pivot_col - first, source * lead - (1.0 - lead))
+        holds = lead.astype(F32)
+        index = jnp.where(mine, pivot_col - first, source * holds - (1.0 - holds))
         slab_copy.wait()
         total = jnp.zeros((block, width), F32)
         for start in range(0, rows, block):
@@ -280,8 +296,8 @@
     def merge():
         core_copy().wait()
         pivot_col = state["pivot_col"]
-        lead = (chip == 0).astype(F32)
-        second = jnp.where((pivot_col >= rows) & (pivot_col < 2 * rows), lead, 0.0)
+        holds = (chip == 0).astype(F32)
+        second = jnp.where((pivot_col >= rows) & (pivot_col < 2 * rows), holds, 0.0)
         mine, theirs = picked[...].astype(F32), picked_in[...].astype(F32)
         even = (core == 0).astype(F32)
         keep_mine = 1.0 - even * second
@@ -408,31 +424,46 @@
 
     def update(piece):
         start, size = pieces[piece]
-        panel = gathered[:, :, start:start + size].reshape(block, size).astype(BF16)
-        product = lax.dot_general(
-            panel, u_ref[...], (((0,), (0,)), ((), ())), preferred_element_type=F32
-        )
-        out_ref[start:start + size, :] = (pivoted[start:start + size, :].astype(F32) - product).astype(BF16)
+
+        def act():
+            panel = gathered[:, :, start:start + size].reshape(block, size).astype(BF16)
+            product = lax.dot_general(
+                panel, u_ref[...], (((0,), (0,)), ((), ())), preferred_element_type=F32
+            )
+            out_ref[start:start + size, :] = (pivoted[start:start + size, :].astype(F32) - product).astype(BF16)
+
+        needed(piece, act)
+        if start < block:
+            @pl.when(lead)
+            def _():
+                end = min(block, start + size)
+                out_ref[start:end, :] = u_ref[start:end, :]
 
     pl.semaphore_wait(barrier, 1 + chips + has_below + has_above)
     panel_copy.wait()
-    pl.when(core == 0)(first_sends)
+    first_sends()
     bookkeeping()
     pick()
     core_copy().start()
-    pl.when(core == 1)(first_sends)
+
     own_homes()
 
     def relays(distance):
         return [relay(distance, piece) for piece in bulk] if distance < length else []
 
     changes = [interchange(start) for start in range(0, rows, block)]
-    plan = inverse[:3] + [merge] + weave(relays(1), [send_rest] + inverse[3:6]) + [own_rest] + inverse[6:8]
-    plan += weave(relays(2), inverse[8:10] + [relay_chips] + inverse[10:]) + [relay_rest(1), assemble, solve]
-    plan += weave(relays(3), changes[:3] + [relay_rest(2)]) + changes[3:]
-    for distance in range(4, length):
-        plan += relays(distance) + [relay_rest(distance - 1)]
-    plan += [relay_rest(length - 1)]
+    plan = inverse[:3] + [merge] + weave(relays(1), inverse[3:6])
+    plan += [other_rest, own_rest(0, other), own_rest(1, x), own_rest(1, other)] + inverse[6:8]
+    second = relays(2)
+    half_way = len(second) // 2
+    plan += weave(second[:half_way], inverse[8:10]) + [pass_rest(1, 1)]
+    plan += weave(second[half_way:], [relay_chips] + inverse[10:])
+    plan += [own_rest(2, x), own_rest(2, other), pass_rest(2, 1), assemble, solve]
+    plan += weave(relays(3), changes[:3] + [pass_rest(2, 2)]) + changes[3:]
+    for distance in range(3, length):
+        plan += relays(distance) if distance > 3 else []
+        plan += [own_rest(distance, x), own_rest(distance, other)]
+        plan += [pass_rest(distance, reach) for reach in range(1, distance + 1)]
     for act in plan:
         act()
 
@@ -441,10 +472,6 @@
         update(piece)
     last_rests()
     update(rest)
-
-    @pl.when(me_r == 0)
-    def _():
-        out_ref[:block, :] = u_ref[...]
 
     drain()
 

time: 28 us -> 25.7 us (0.918)
  Pallas kernels: 26.6 us -> 24.2 us
    pallas_call x1, Pallas kernels: 26.6 us -> 24.2 us  [per_device(): pl.pallas_call(functools.partial(kernel, n_prow, n_pcol), out_shape=pltpu...]
where the time goes in v2:
time: 25.7 us; the launch traced here: 25.4 us
  Pallas kernels  24.2 us (94%)
  local copies, waits for them, and re-layouts  1.15 us (4%)
    pallas_call x1, Pallas kernels, per_device(): pl.pallas_call(functools.partial(kernel, n_prow, n_pcol), out_shape=pltpu...  24.2 us
    unnamed x1, local copies, waits for them, and re-layouts  1.15 us

profile of v2, /device:TPU:0, one launch (start us, length us, event | category | flops | bytes accessed | tf_op | source)
XLA Modules:
  0.0 25.4 jit_solution(10363128820714172198)
XLA Ops:
  0.0 24.2 %shard_map.46 = bf16[2048,384]{1,0:T(8,128)(2,1)S(1)} custom-call(bf16[2048,384]{1,0:T(8,128)(2,1)} %slab_hbm.1, s32[1,512]{1,0:T(1,128)} %bitcast.1, bf16[512,512]{1,0:T(8,128)(2,1)} %l_top_hbm.1, bf16[64,2048]{1,0:T(8,128)(2,1)} %panel_hbm.1), custom_call_target="tpu_custom_call" | custom-call | tf_op jit(solution)/shard_map/pallas_call | solution.py:490
  24.2 1.1 %copy.6 = bf16[2048,384]{1,0:T(8,128)(2,1)} copy(bf16[2048,384]{1,0:T(8,128)(2,1)S(1)} %shard_map.46) | data formatting | bytes 3145728

commit v3 on v2

--- a/solution.py
+++ b/solution.py
@@ -38,6 +38,8 @@
 
 
 EDGES = (0, 4, 8, 11, 13, 16)
+LATE = 3
+LIMIT = 54 * 2**20
 
 
 def cuts(width):
@@ -53,11 +55,20 @@
     return plan
 
 
+def late_pieces(block, width):
+    pieces = cuts(width)
+    return [piece for piece in range(LATE, len(pieces)) if pieces[piece][0] >= block]
+
+
+def trailing(panel, u, rows):
+    product = lax.dot_general(panel, u, (((0,), (0,)), ((), ())), preferred_element_type=F32)
+    return (rows.astype(F32) - product).astype(BF16)
+
+
 def kernel(
     n_prow, n_pcol,
-    slab_hbm, pivots_hbm, l_top_hbm, panel_hbm, out_ref,
-    slab_ref, pivots_ref, l_top_ref, gathered, picked, picked_in, merged, homes, pivoted, inverse_hi, inverse_lo, high,
-    u_ref,
+    slab_hbm, pivots_hbm, l_top_hbm, panel_hbm, out_ref, gathered, pivoted, u_ref,
+    slab_ref, pivots_ref, l_top_ref, picked, picked_in, merged, homes, inverse_hi, inverse_lo, high,
     local_sem, line_recv, cross_recv, rest_recv, sent, core_sem, chip_send, chip_recv, relay_send, relay_recv,
 ):
     block = l_top_ref.shape[0]
@@ -427,10 +438,7 @@
 
         def act():
             panel = gathered[:, :, start:start + size].reshape(block, size).astype(BF16)
-            product = lax.dot_general(
-                panel, u_ref[...], (((0,), (0,)), ((), ())), preferred_element_type=F32
-            )
-            out_ref[start:start + size, :] = (pivoted[start:start + size, :].astype(F32) - product).astype(BF16)
+            out_ref[start:start + size, :] = trailing(panel, u_ref[...], pivoted[start:start + size, :])
 
         needed(piece, act)
         if start < block:
@@ -467,13 +475,38 @@
     for act in plan:
         act()
 
+    late = late_pieces(block, rows)
     for piece in bulk:
         crossed(piece)
-        update(piece)
+        if piece not in late:
+            update(piece)
     last_rests()
-    update(rest)
+    if rest not in late:
+        update(rest)
 
     drain()
+
+
+def finish(done_ref, gathered, pivoted, u_ref, out_hbm, result, sem):
+    block = u_ref.shape[0]
+    pieces = cuts(gathered.shape[2])
+    late = late_pieces(block, gathered.shape[2])
+    early = pieces[late[0]][0] if late else gathered.shape[2]
+    copies = []
+
+    def store(source, first, size):
+        copy = pltpu.make_async_copy(source.at[pl.ds(first, size)], out_hbm.at[pl.ds(first, size)], sem.at[len(copies)])
+        copy.start()
+        copies.append(copy)
+
+    store(done_ref, 0, early)
+    for piece in late:
+        start, size = pieces[piece]
+        panel = gathered[:, :, start:start + size].reshape(block, size).astype(BF16)
+        result[start:start + size, :] = trailing(panel, u_ref[...], pivoted[start:start + size, :])
+        store(result, start, size)
+    for copy in copies:
+        copy.wait()
 
 
 def per_device(n_prow, n_pcol, slab, pivots, l_top, l_panel_t):
@@ -487,25 +520,28 @@
     vmem = pl.BlockSpec(memory_space=pltpu.VMEM)
     anywhere = pl.BlockSpec(memory_space=pltpu.HBM)
     dma = pltpu.SemaphoreType.DMA
-    return pl.pallas_call(
+    kept = [
+        pltpu.VMEM((rows, width), BF16),
+        pltpu.VMEM((n_pcol, depth, rows), kind),
+        pltpu.VMEM((rows, width), BF16),
+        pltpu.VMEM((block, width), BF16),
+    ]
+    done, gathered, pivoted, u = pl.pallas_call(
         functools.partial(kernel, n_prow, n_pcol),
-        out_shape=pltpu.VMEM((rows, width), BF16),
+        out_shape=kept,
         in_specs=[anywhere] * 4,
-        out_specs=vmem,
+        out_specs=[vmem] * 4,
         scratch_shapes=[
             pltpu.VMEM((rows, width), BF16),
             pltpu.VMEM((1, block), jnp.int32),
             pltpu.VMEM((block, block), BF16),
-            pltpu.VMEM((n_pcol, depth, rows), kind),
             pltpu.VMEM((block, width), BF16),
             pltpu.VMEM((block, width), BF16),
             pltpu.VMEM((chips, block, width), BF16),
             pltpu.VMEM((block, width + LANES), BF16),
-            pltpu.VMEM((rows, width), BF16),
             pltpu.VMEM((block, block), BF16),
             pltpu.VMEM((block, block), BF16),
             pltpu.VMEM((block, block), F32),
-            pltpu.VMEM((block, width), BF16),
             dma((4,)),
             dma((n_pcol // 2, n_pieces - 1)),
             dma((n_pieces - 1,)),
@@ -517,8 +553,16 @@
             dma((chips - 1,)),
             dma((chips - 1,)),
         ],
-        compiler_params=pltpu.CompilerParams(collective_id=0, has_side_effects=True, vmem_limit_bytes=60 * 2**20),
+        compiler_params=pltpu.CompilerParams(collective_id=0, has_side_effects=True, vmem_limit_bytes=LIMIT),
     )(slab, pivots.reshape(1, block), l_top, panel)
+    return pl.pallas_call(
+        finish,
+        out_shape=pltpu.HBM((rows, width), BF16),
+        in_specs=[vmem] * 4,
+        out_specs=anywhere,
+        scratch_shapes=[pltpu.VMEM((rows, width), BF16), dma((n_pieces,))],
+        compiler_params=pltpu.CompilerParams(vmem_limit_bytes=16 * 2**20),
+    )(done, gathered, pivoted, u)
 
 
 def solution(mesh):

time: 25.7 us -> 25.4 us (0.988)
  local copies, waits for them, and re-layouts: 1.15 us -> 0 us
  Pallas kernels: 24.2 us -> 25.1 us
    unnamed x1 -> x0, local copies, waits for them, and re-layouts: 1.15 us -> none
    pallas_call x1 -> x2, Pallas kernels: 24.2 us -> 25.1 us  [the longest x1 23.8 us: per_device(): pl.pallas_call(functools.partial(kernel, n_prow, n_pcol), out_shape=kept,...]
where the time goes in v3:
time: 25.4 us; the launch traced here: 25.1 us
  Pallas kernels  25.1 us (99%)
    pallas_call x1, Pallas kernels, per_device(): pl.pallas_call(functools.partial(kernel, n_prow, n_pcol), out_shape=kept,...  23.8 us
    pallas_call x1, Pallas kernels, per_device(): pl.pallas_call(finish, out_shape=pltpu.HBM((rows, width), BF16), in_specs...  1.32 us

profile of v3, /device:TPU:0, one launch (start us, length us, event | category | flops | bytes accessed | tf_op | source)
XLA Modules:
  0.0 25.1 jit_solution(4056441380616720200)
XLA Ops:
  0.0 23.8 %shard_map.46 = (bf16[2048,384]{1,0:T(8,128)(2,1)S(1)}, bf16[8,64,2048]{2,1,0:T(8,128)(2,1)S(1)}, bf16[2048,384]{1,0:T(8,128)(2,1)S(1)}, bf16[512,384]{1,0:T(8,128)(2,1)S(1)}) custom-call(bf16[2048,384]{1,0:T(8,128)(2,1)} %slab_hbm.1, s32[1,512]{1,0:T(1,128)} %bitcast.1, bf16[512,512]{1,0:T(8,128)(2,1)} %l_top_hbm.1, bf16[64,2048]{1,0:T(8,128)(2,1)} %panel_hbm.1), custom_call_target="tpu_custom_call" | custom-call | tf_op jit(solution)/shard_map/pallas_call | solution.py:529
  23.8 1.3 %shard_map.47 = bf16[2048,384]{1,0:T(8,128)(2,1)} custom-call(bf16[2048,384]{1,0:T(8,128)(2,1)S(1)} %get-tuple-element.9.done_ref, bf16[8,64,2048]{2,1,0:T(8,128)(2,1)S(1)} %get-tuple-element.10.gathered, bf16[2048,384]{1,0:T(8,128)(2,1)S(1)} %get-tuple-element.11.pivoted, bf16[512,384]{1,0:T(8,128)(2,1)S(1)} %get-tuple-element.12.u_ref), custom_call_target="tpu_custom_call" | custom-call | tf_op jit(solution)/shard_map/pallas_call | solution.py:558

commit v4 on v3

--- a/solution.py
+++ b/solution.py
@@ -37,15 +37,36 @@
     return dot(a_high, b_high) + (dot(a_high, b_low) + dot(a_low, b_high))
 
 
-EDGES = (0, 4, 8, 11, 13, 16)
-LATE = 3
+STRIPS = (0, 4, 7, 10)
+THICK = 12
+THIN = 14
 LIMIT = 54 * 2**20
 
 
-def cuts(width):
+def cuts(width, thick=True):
     units = width // LANES
-    edges = [(units * part) // 16 * LANES for part in EDGES]
+    edges = [units * part // 16 * LANES for part in STRIPS + (THICK if thick else THIN, 16)]
     return [(a, b - a) for a, b in zip(edges[:-1], edges[1:])]
+
+
+def box(columns, shape):
+    for count in range(1, shape[0] + 1):
+        if columns % (count * LANES) == 0 and columns // count <= shape[2]:
+            return count, columns // count
+
+
+def level_of(gathered, u_ref, level, columns):
+    depth = 2 * gathered.shape[1]
+    panel = gathered[pl.ds(level * 2, 2), :, columns[0]:columns[0] + columns[1]].reshape(depth, columns[1])
+    return lax.dot_general(
+        panel.astype(BF16), u_ref[pl.ds(pl.multiple_of(level * depth, depth), depth), :],
+        (((0,), (0,)), ((), ())), preferred_element_type=F32,
+    )
+
+
+def last_level(length):
+    z = lax.axis_index("pcol") // 2
+    return jnp.where(z < length // 2, length - 1, 0)
 
 
 def weave(events, work):
@@ -55,11 +76,6 @@
     return plan
 
 
-def late_pieces(block, width):
-    pieces = cuts(width)
-    return [piece for piece in range(LATE, len(pieces)) if pieces[piece][0] >= block]
-
-
 def trailing(panel, u, rows):
     product = lax.dot_general(panel, u, (((0,), (0,)), ((), ())), preferred_element_type=F32)
     return (rows.astype(F32) - product).astype(BF16)
@@ -67,7 +83,7 @@
 
 def kernel(
     n_prow, n_pcol,
-    slab_hbm, pivots_hbm, l_top_hbm, panel_hbm, out_ref, gathered, pivoted, u_ref,
+    slab_hbm, pivots_hbm, l_top_hbm, panel_hbm, out_ref, gathered, u_ref, partial, pivoted,
     slab_ref, pivots_ref, l_top_ref, picked, picked_in, merged, homes, inverse_hi, inverse_lo, high,
     local_sem, line_recv, cross_recv, rest_recv, sent, core_sem, chip_send, chip_recv, relay_send, relay_recv,
 ):
@@ -125,42 +141,70 @@
     has_below = (z + length - 1) // length
     has_above = (2 * length - 2 - z) // length
 
-    def strip(source, piece):
-        start, size = pieces[piece]
-        return gathered.at[source, :, pl.ds(start, size)]
-
-    def send(part, send_sem, recv_sem, target):
+    tail = rest - 1
+    mixed = length == 4
+
+    def by_class(at, act):
+        if mixed:
+            outer = ((at == 0) | (at == length - 1)) & jnp.logical_not(lead)
+            pl.when(outer)(lambda: act(True))
+            pl.when(jnp.logical_not(outer))(lambda: act(False))
+        else:
+            act(True)
+
+    def columns_of(piece, thick):
+        return cuts(gathered.shape[2], thick)[piece]
+
+    def send(source, columns, send_sem, recv_sem, target):
+        part = gathered.at[source, :, pl.ds(*columns)]
+        pltpu.make_async_remote_copy(
+            src_ref=part, dst_ref=part, send_sem=send_sem, recv_sem=recv_sem,
+            device_id=(me_r, target), device_id_type=MESH,
+        ).start()
+
+    def arrival(columns, send_sem, recv_sem):
+        count, size = box(columns, gathered.shape)
+        part = gathered.at[pl.ds(0, count), :, pl.ds(0, size)]
         return pltpu.make_async_remote_copy(
             src_ref=part, dst_ref=part, send_sem=send_sem, recv_sem=recv_sem,
-            device_id=(me_r, target), device_id_type=MESH,
+            device_id=(me_r, z * 2 + other), device_id_type=MESH,
         )
 
-    def line(way, at, piece):
-        target = me_c + 2 - 4 * way
-        return send(strip(at * 2 + x, piece), sent.at[way], line_recv.at[at, piece], target)
-
-    def line_rest(way, at, side):
-        target = me_c + 2 - 4 * way
-        return send(strip(at * 2 + side, rest), sent.at[2 + way], rest_recv.at[at, side], target)
-
-    def cross(at, piece):
-        return send(strip(at * 2 + x, piece), sent.at[4], cross_recv.at[piece], z * 2 + other)
-
-    def cross_rest():
-        return send(strip(me_c, rest), sent.at[5], rest_recv.at[z, x], z * 2 + other)
-
-    def both_ways(start):
-        pl.when(z < length - 1)(lambda: start(0))
-        pl.when(z > 0)(lambda: start(1))
+    def landed(columns, recv_sem):
+        arrival(columns, sent.at[0], recv_sem).wait_recv()
+
+    def neighbour(way):
+        return me_c + 2 - 4 * way
+
+    def line(way, at, piece, thick):
+        send(at * 2 + x, columns_of(piece, thick), sent.at[way], line_recv.at[at, piece], neighbour(way))
+
+    def cross(at, piece, thick):
+        send(at * 2 + x, columns_of(piece, thick), sent.at[4], cross_recv.at[piece], z * 2 + other)
+
+    def line_rest(way, at, side, thick):
+        send(at * 2 + side, columns_of(rest, thick), sent.at[2 + way], rest_recv.at[at], neighbour(way))
+
+    def classed(at, piece, act):
+        if piece >= tail:
+            by_class(at, act)
+        else:
+            act(True)
+
+    def both_ways(act):
+        pl.when(z < length - 1)(lambda: act(0))
+        pl.when(z > 0)(lambda: act(1))
 
     def first_sends():
         for piece in bulk:
-            def own():
-                both_ways(lambda way: line(way, z, piece).start())
-                cross(z, piece).start()
-            needed(piece, own)
-            if piece == rest // 2:
-                cross_rest().start()
+            def own(thick):
+                both_ways(lambda way: line(way, z, piece, thick))
+                cross(z, piece, thick)
+            needed(piece, lambda: classed(z, piece, own))
+            if piece == 0:
+                by_class(z, lambda thick: send(
+                    me_c, columns_of(rest, thick), sent.at[5], rest_recv.at[z], z * 2 + other
+                ))
         own_rest(0, x)()
 
     def rest_ways(distance, act):
@@ -169,17 +213,25 @@
             pl.when(z == length - 1 - distance)(lambda: act(1))
 
     def own_rest(distance, side):
-        return lambda: rest_ways(distance, lambda way: line_rest(way, z, side).start())
+        def act(way):
+            by_class(z, lambda thick: line_rest(way, z, side, thick))
+        return lambda: rest_ways(distance, act)
 
     def other_rest():
-        send(strip(z * 2 + other, rest), sent.at[5], rest_recv.at[z, other], z * 2 + other).wait_recv()
+        by_class(z, lambda thick: landed(columns_of(rest, thick)[1], rest_recv.at[z]))
+
+    def both_rests(at, act=None):
+        def classed_act(thick):
+            landed(2 * columns_of(rest, thick)[1], rest_recv.at[at])
+            if act is not None:
+                for side in (0, 1):
+                    act(side, thick)
+        by_class(at, classed_act)
 
     def pass_rest(distance, reach):
         def onward(way):
             at = z + (2 * way - 1) * reach
-            for side in (0, 1):
-                line_rest(way, at, side).wait_recv()
-                line_rest(way, at, side).start()
+            both_rests(at, lambda side, thick: line_rest(way, at, side, thick))
         return lambda: rest_ways(distance, onward)
 
     def relay(distance, piece):
@@ -188,54 +240,58 @@
                 (0, z - distance, z >= distance, z < length - 1),
                 (1, z + distance, z < length - distance, z > 0),
             ):
-                @pl.when(reached)
-                def _():
-                    line(way, at, piece).wait_recv()
-                    pl.when(onward)(lambda: line(way, at, piece).start())
-                    cross(at, piece).start()
+                def pass_on(thick):
+                    landed(columns_of(piece, thick)[1], line_recv.at[at, piece])
+                    pl.when(onward)(lambda: line(way, at, piece, thick))
+                    cross(at, piece, thick)
+
+                pl.when(reached)(lambda: classed(at, piece, pass_on))
         return lambda: needed(piece, both)
 
-    def last_rests():
-        for distance in range(1, length):
-            for way, at, reached in (
-                (0, z - distance, (z >= distance) & (z == length - 1)),
-                (1, z + distance, (z < length - distance) & (z == 0)),
-            ):
-                @pl.when(reached)
-                def _():
-                    for side in (0, 1):
-                        line_rest(way, at, side).wait_recv()
+    def last_rests(distance):
+        for way, at, reached in (
+            (0, z - distance, (z >= distance) & (z == length - 1)),
+            (1, z + distance, (z < length - distance) & (z == 0)),
+        ):
+            pl.when(reached)(lambda: both_rests(at))
+
+    def lanes_of(pieces_of, levels, leading):
+        total = 0
+        for at in levels:
+            thick = not mixed or (not leading and at in (0, length - 1))
+            for piece in pieces_of:
+                start, size = columns_of(piece, thick)
+                total += 0 if leading and start + size <= block else size
+        return total
+
+    def for_lead(act):
+        pl.when(lead)(lambda: act(True))
+        pl.when(jnp.logical_not(lead))(lambda: act(False))
 
     def crossed(piece):
-        start, size = pieces[piece]
-        every = gathered.at[pl.ds(0, length), :, pl.ds(start, size)]
-        needed(piece, lambda: send(every, sent.at[4], cross_recv.at[piece], z * 2 + other).wait_recv())
+        if piece == tail:
+            for_lead(lambda leading: landed(lanes_of([tail], range(length), leading), cross_recv.at[tail]))
+        else:
+            needed(piece, lambda: landed(length * pieces[piece][1], cross_recv.at[piece]))
 
     def drain():
-        thin = pieces[rest][1]
-
-        def gone(sem, count, size):
-            part = gathered.at[pl.ds(0, count), :, pl.ds(0, size)]
-            send(part, sent.at[sem], rest_recv.at[0, 0], z * 2 + other).wait_send()
-
-        def gone_bulk(sem, count):
-            def wide(first):
-                return sum(size for start, size in pieces[:-1] if start + size > first)
-
-            pl.when(lead)(lambda: gone(sem, count, wide(block)))
-            pl.when(jnp.logical_not(lead))(lambda: gone(sem, count, wide(0)))
-
-        def gone_line(way, count):
-            gone_bulk(way, count)
-            gone(2 + way, count, 2 * thin)
-
-        for at in range(length):
-            if at < length - 1:
-                pl.when(z == at)(lambda: gone_line(0, at + 1))
-            if at > 0:
-                pl.when(z == at)(lambda: gone_line(1, length - at))
-        gone_bulk(4, length)
-        gone(5, 1, thin)
+        def gone(sem, columns):
+            arrival(columns, sent.at[sem], rest_recv.at[0]).wait_send()
+
+        def act(leading):
+            for at in range(length):
+                def here():
+                    if at < length - 1:
+                        gone(0, lanes_of(bulk, range(at + 1), leading))
+                        gone(2, 2 * lanes_of([rest], range(at + 1), leading))
+                    if at > 0:
+                        gone(1, lanes_of(bulk, range(at, length), leading))
+                        gone(3, 2 * lanes_of([rest], range(at, length), leading))
+                    gone(5, lanes_of([rest], [at], leading))
+                pl.when(z == at)(here)
+            gone(4, lanes_of(bulk, range(length), leading))
+
+        for_lead(act)
 
     state = {}
     ii = iota((block, block), 0)
@@ -475,36 +531,41 @@
     for act in plan:
         act()
 
-    late = late_pieces(block, rows)
     for piece in bulk:
+        if piece == 0:
+            for distance in range(1, length - 1):
+                last_rests(distance)
+            start, size = columns_of(rest, False)
+            total = pivoted[start:start + size, :].astype(F32)
+            last = last_level(length)
+            for step in range(1, length):
+                total = total - level_of(gathered, u_ref, (last + step) % length, (start, size))
+            partial[...] = total
         crossed(piece)
-        if piece not in late:
+        if piece < tail:
             update(piece)
-    last_rests()
-    if rest not in late:
-        update(rest)
+    last_rests(length - 1)
 
     drain()
 
 
-def finish(done_ref, gathered, pivoted, u_ref, out_hbm, result, sem):
+def finish(done_ref, gathered, u_ref, partial, pivoted, out_hbm, result, sem):
     block = u_ref.shape[0]
-    pieces = cuts(gathered.shape[2])
-    late = late_pieces(block, gathered.shape[2])
-    early = pieces[late[0]][0] if late else gathered.shape[2]
-    copies = []
-
-    def store(source, first, size):
-        copy = pltpu.make_async_copy(source.at[pl.ds(first, size)], out_hbm.at[pl.ds(first, size)], sem.at[len(copies)])
+    edge = cuts(gathered.shape[2])[-2][0]
+    start, size = cuts(gathered.shape[2], False)[-1]
+
+    def store(source, start, size, n):
+        copy = pltpu.make_async_copy(source, out_hbm.at[pl.ds(start, size)], sem.at[n])
         copy.start()
-        copies.append(copy)
-
-    store(done_ref, 0, early)
-    for piece in late:
-        start, size = pieces[piece]
-        panel = gathered[:, :, start:start + size].reshape(block, size).astype(BF16)
-        result[start:start + size, :] = trailing(panel, u_ref[...], pivoted[start:start + size, :])
-        store(result, start, size)
+        return copy
+
+    copies = [store(done_ref.at[pl.ds(0, edge)], 0, edge, 0)]
+    panel = gathered[:, :, edge:start].reshape(block, start - edge).astype(BF16)
+    result[:start - edge, :] = trailing(panel, u_ref[...], pivoted[edge:start, :])
+    copies.append(store(result.at[pl.ds(0, start - edge)], edge, start - edge, 2))
+    last = last_level(gathered.shape[0] // 2)
+    result[start - edge:, :] = (partial[...] - level_of(gathered, u_ref, last, (start, size))).astype(BF16)
+    copies.append(store(result.at[pl.ds(start - edge, size)], start, size, 1))
     for copy in copies:
         copy.wait()
 
@@ -523,14 +584,15 @@
     kept = [
         pltpu.VMEM((rows, width), BF16),
         pltpu.VMEM((n_pcol, depth, rows), kind),
+        pltpu.VMEM((block, width), BF16),
+        pltpu.VMEM((cuts(rows, False)[-1][1], width), F32),
         pltpu.VMEM((rows, width), BF16),
-        pltpu.VMEM((block, width), BF16),
     ]
-    done, gathered, pivoted, u = pl.pallas_call(
+    done, gathered, u, partial, pivoted = pl.pallas_call(
         functools.partial(kernel, n_prow, n_pcol),
         out_shape=kept,
         in_specs=[anywhere] * 4,
-        out_specs=[vmem] * 4,
+        out_specs=[vmem] * 5,
         scratch_shapes=[
             pltpu.VMEM((rows, width), BF16),
             pltpu.VMEM((1, block), jnp.int32),
@@ -545,7 +607,7 @@
             dma((4,)),
             dma((n_pcol // 2, n_pieces - 1)),
             dma((n_pieces - 1,)),
-            dma((n_pcol // 2, 2)),
+            dma((n_pcol // 2,)),
             dma((6,)),
             dma((2,)),
             dma((chips - 1,)),
@@ -558,11 +620,11 @@
     return pl.pallas_call(
         finish,
         out_shape=pltpu.HBM((rows, width), BF16),
-        in_specs=[vmem] * 4,
+        in_specs=[vmem] * 5,
         out_specs=anywhere,
-        scratch_shapes=[pltpu.VMEM((rows, width), BF16), dma((n_pieces,))],
+        scratch_shapes=[pltpu.VMEM((rows - cuts(rows)[-2][0], width), BF16), dma((3,))],
         compiler_params=pltpu.CompilerParams(vmem_limit_bytes=16 * 2**20),
-    )(done, gathered, pivoted, u)
+    )(done, gathered, u, partial, pivoted)
 
 
 def solution(mesh):

time: 25.4 us -> 25.1 us (0.988)
  the two profiles are of different devices: /device:TPU:0 before, /device:TPU:4 now
where the time goes in v4:
time: 25.1 us; the launch traced here: 24.9 us
  Pallas kernels  24.9 us (99%)
    pallas_call x1, Pallas kernels, per_device(): pl.pallas_call(functools.partial(kernel, n_prow, n_pcol), out_shape=kept,...  23.6 us
    pallas_call x1, Pallas kernels, per_device(): pl.pallas_call(finish, out_shape=pltpu.HBM((rows, width), BF16), in_specs...  1.31 us

profile of v4, /device:TPU:4, one launch (start us, length us, event | category | flops | bytes accessed | tf_op | source)
XLA Modules:
  0.0 24.9 jit_solution(9127176117036736761)
XLA Ops:
  0.0 23.6 %shard_map.46 = (bf16[2048,384]{1,0:T(8,128)(2,1)S(1)}, bf16[8,64,2048]{2,1,0:T(8,128)(2,1)S(1)}, bf16[512,384]{1,0:T(8,128)(2,1)S(1)}, f32[256,384]{1,0:T(8,128)S(1)}, bf16[2048,384]{1,0:T(8,128)(2,1)S(1)}) custom-call(bf16[2048,384]{1,0:T(8,128)(2,1)} %slab_hbm.1, s32[1,512]{1,0:T(1,128)} %bitcast.1, bf16[512,512]{1,0:T(8,128)(2,1)} %l_top_hbm.1, ...), custom_call_target="tpu_custom_call" | custom-call | tf_op jit(solution)/shard_map/pallas_call | solution.py:591
  23.6 1.3 %shard_map.47 = bf16[2048,384]{1,0:T(8,128)(2,1)} custom-call(bf16[2048,384]{1,0:T(8,128)(2,1)S(1)} %get-tuple-element.10.done_ref, bf16[8,64,2048]{2,1,0:T(8,128)(2,1)S(1)} %get-tuple-element.11.gathered, bf16[512,384]{1,0:T(8,128)(2,1)S(1)} %get-tuple-element.12.u_ref, f32[256,384]{1,0:T(8,128)S(1)} %get-tuple-element.13.partial, ...), custom_call_target="tpu_custom_call" | custom-call | tf_op jit(solution)/shard_map/pallas_call | solution.py:620

commit v5 on v4

--- a/solution.py
+++ b/solution.py
@@ -84,8 +84,8 @@
 def kernel(
     n_prow, n_pcol,
     slab_hbm, pivots_hbm, l_top_hbm, panel_hbm, out_ref, gathered, u_ref, partial, pivoted,
-    slab_ref, pivots_ref, l_top_ref, picked, picked_in, merged, homes, inverse_hi, inverse_lo, high,
-    local_sem, line_recv, cross_recv, rest_recv, sent, core_sem, chip_send, chip_recv, relay_send, relay_recv,
+    slab_ref, pivots_ref, l_top_ref, picked, picked_in, merged, homes, inverse_hi, inverse_lo, high, guest,
+    local_sem, line_recv, cross_recv, rest_recv, sent, guest_sem, ready, core_sem, chip_send, chip_recv, relay_send, relay_recv,
 ):
     block = l_top_ref.shape[0]
     rows, width = slab_ref.shape
@@ -143,6 +143,8 @@
 
     tail = rest - 1
     mixed = length == 4
+    moves = n_prow == 4 and length <= 4
+    giver = me_r == 2
 
     def by_class(at, act):
         if mixed:
@@ -152,8 +154,10 @@
         else:
             act(True)
 
-    def columns_of(piece, thick):
-        return cuts(gathered.shape[2], thick)[piece]
+    def columns_of(piece, kind):
+        thick, given = kind if isinstance(kind, tuple) else (kind, False)
+        start, size = cuts(gathered.shape[2], thick)[piece]
+        return (start + LANES, size - LANES) if given and piece == tail else (start, size)
 
     def send(source, columns, send_sem, recv_sem, target):
         part = gathered.at[source, :, pl.ds(*columns)]
@@ -177,7 +181,7 @@
         return me_c + 2 - 4 * way
 
     def line(way, at, piece, thick):
-        send(at * 2 + x, columns_of(piece, thick), sent.at[way], line_recv.at[at, piece], neighbour(way))
+        send(at * 2 + x, columns_of(piece, thick), sent.at[way if piece < 2 else 2 + way], line_recv.at[at, piece], neighbour(way))
 
     def cross(at, piece, thick):
         send(at * 2 + x, columns_of(piece, thick), sent.at[4], cross_recv.at[piece], z * 2 + other)
@@ -186,7 +190,10 @@
         send(at * 2 + side, columns_of(rest, thick), sent.at[2 + way], rest_recv.at[at], neighbour(way))
 
     def classed(at, piece, act):
-        if piece >= tail:
+        if piece == tail and moves:
+            pl.when(giver)(lambda: by_class(at, lambda thick: act((thick, True))))
+            pl.when(jnp.logical_not(giver))(lambda: by_class(at, act))
+        elif piece >= tail:
             by_class(at, act)
         else:
             act(True)
@@ -195,7 +202,89 @@
         pl.when(z < length - 1)(lambda: act(0))
         pl.when(z > 0)(lambda: act(1))
 
+    moved = pl.ds(pieces[tail][0], LANES)
+
+    def guest_copy(source, target, recv_sem, row, column):
+        return pltpu.make_async_remote_copy(
+            src_ref=source, dst_ref=target, send_sem=guest_sem.at[4], recv_sem=recv_sem,
+            device_id=(row, column), device_id_type=MESH,
+        )
+
+    def guest_total(count, recv_sem):
+        rows_of, size = box(count * LANES, gathered.shape)
+        part = gathered.at[pl.ds(0, rows_of), :, pl.ds(0, size)]
+        return guest_copy(part, part, recv_sem, me_r, z * 2 + other)
+
+    def only(who):
+        return lambda act: pl.when(who)(act) if moves else None
+
+    def guest_give():
+        @only(giver)
+        def _():
+            guest_copy(gathered.at[me_c, :, moved], guest.at[me_c], guest_sem.at[0], 0, me_c).start()
+
+    def guest_cross(source):
+        part = guest.at[source]
+        guest_copy(part, part, guest_sem.at[2], me_r, z * 2 + other).start()
+
+    def guest_home(source):
+        guest_copy(guest.at[source], gathered.at[source, :, moved], guest_sem.at[3], 2, me_c).start()
+
+    def tell(n):
+        @only(lead)
+        def _():
+            both_ways(lambda way: pl.semaphore_signal(
+                ready.at[n], inc=1, device_id=(0, neighbour(way)), device_id_type=MESH
+            ))
+
+    def told(n):
+        @only(lead)
+        def _():
+            pl.semaphore_wait(ready.at[n], has_below + has_above)
+
+    def guest_own():
+        told(1)
+
+        @only(lead)
+        def _():
+            guest_total(1, guest_sem.at[0]).wait_recv()
+            part = guest.at[me_c]
+            for step in range(1, length):
+                guest_copy(part, part, guest_sem.at[1], me_r, (z + step) % length * 2 + x).start()
+            guest_cross(me_c)
+
+    def guest_line():
+        @only(lead)
+        def _():
+            guest_total(length - 1, guest_sem.at[1]).wait_recv()
+            for step in range(1, length):
+                guest_cross((z + step) % length * 2 + x)
+            for step in range(1, length):
+                guest_home((z + step) % length * 2 + x)
+
+    def guest_other():
+        @only(lead)
+        def _():
+            guest_total(length, guest_sem.at[2]).wait_recv()
+            for at in range(length):
+                guest_home(at * 2 + other)
+
+    def guest_last():
+        @only(giver)
+        def _():
+            guest_total(2 * length - 1, guest_sem.at[3]).wait_recv()
+
+    def guest_drain():
+        @only(giver)
+        def _():
+            guest_total(1, guest_sem.at[3]).wait_send()
+
+        @only(lead)
+        def _():
+            guest_total(4 * length - 2, guest_sem.at[3]).wait_send()
+
     def first_sends():
+        guest_give()
         for piece in bulk:
             def own(thick):
                 both_ways(lambda way: line(way, z, piece, thick))
@@ -255,22 +344,27 @@
         ):
             pl.when(reached)(lambda: both_rests(at))
 
-    def lanes_of(pieces_of, levels, leading):
+    def lanes_of(pieces_of, levels, kind):
+        leading, given = kind
         total = 0
         for at in levels:
             thick = not mixed or (not leading and at in (0, length - 1))
             for piece in pieces_of:
-                start, size = columns_of(piece, thick)
+                start, size = columns_of(piece, (thick, given))
                 total += 0 if leading and start + size <= block else size
         return total
 
-    def for_lead(act):
-        pl.when(lead)(lambda: act(True))
-        pl.when(jnp.logical_not(lead))(lambda: act(False))
+    def for_kinds(act):
+        pl.when(lead)(lambda: act((True, False)))
+        if moves:
+            pl.when(giver)(lambda: act((False, True)))
+            pl.when(jnp.logical_not(lead | giver))(lambda: act((False, False)))
+        else:
+            pl.when(jnp.logical_not(lead))(lambda: act((False, False)))
 
     def crossed(piece):
         if piece == tail:
-            for_lead(lambda leading: landed(lanes_of([tail], range(length), leading), cross_recv.at[tail]))
+            for_kinds(lambda kind: landed(lanes_of([tail], range(length), kind), cross_recv.at[tail]))
         else:
             needed(piece, lambda: landed(length * pieces[piece][1], cross_recv.at[piece]))
 
@@ -278,20 +372,21 @@
         def gone(sem, columns):
             arrival(columns, sent.at[sem], rest_recv.at[0]).wait_send()
 
-        def act(leading):
+        def act(kind):
             for at in range(length):
                 def here():
                     if at < length - 1:
-                        gone(0, lanes_of(bulk, range(at + 1), leading))
-                        gone(2, 2 * lanes_of([rest], range(at + 1), leading))
+                        gone(0, lanes_of(range(2), range(at + 1), kind))
+                        gone(2, lanes_of([*range(2, rest), rest, rest], range(at + 1), kind))
                     if at > 0:
-                        gone(1, lanes_of(bulk, range(at, length), leading))
-                        gone(3, 2 * lanes_of([rest], range(at, length), leading))
-                    gone(5, lanes_of([rest], [at], leading))
+                        gone(1, lanes_of(range(2), range(at, length), kind))
+                        gone(3, lanes_of([*range(2, rest), rest, rest], range(at, length), kind))
+                    gone(5, lanes_of([rest], [at], kind))
                 pl.when(z == at)(here)
-            gone(4, lanes_of(bulk, range(length), leading))
-
-        for_lead(act)
+            gone(4, lanes_of(bulk, range(length), kind))
+
+        for_kinds(act)
+        guest_drain()
 
     state = {}
     ii = iota((block, block), 0)
@@ -506,9 +601,12 @@
     pl.semaphore_wait(barrier, 1 + chips + has_below + has_above)
     panel_copy.wait()
     first_sends()
+    tell(0)
     bookkeeping()
     pick()
     core_copy().start()
+    told(0)
+    tell(1)
 
     own_homes()
 
@@ -516,14 +614,14 @@
         return [relay(distance, piece) for piece in bulk] if distance < length else []
 
     changes = [interchange(start) for start in range(0, rows, block)]
-    plan = inverse[:3] + [merge] + weave(relays(1), inverse[3:6])
+    plan = inverse[:3] + [merge, guest_own] + weave(relays(1), inverse[3:6])
     plan += [other_rest, own_rest(0, other), own_rest(1, x), own_rest(1, other)] + inverse[6:8]
     second = relays(2)
     half_way = len(second) // 2
-    plan += weave(second[:half_way], inverse[8:10]) + [pass_rest(1, 1)]
+    plan += weave(second[:half_way], inverse[8:10]) + [guest_line, pass_rest(1, 1)]
     plan += weave(second[half_way:], [relay_chips] + inverse[10:])
     plan += [own_rest(2, x), own_rest(2, other), pass_rest(2, 1), assemble, solve]
-    plan += weave(relays(3), changes[:3] + [pass_rest(2, 2)]) + changes[3:]
+    plan += weave(relays(3), changes[:3] + [pass_rest(2, 2)]) + changes[3:] + [guest_other]
     for distance in range(3, length):
         plan += relays(distance) if distance > 3 else []
         plan += [own_rest(distance, x), own_rest(distance, other)]
@@ -545,6 +643,7 @@
         if piece < tail:
             update(piece)
     last_rests(length - 1)
+    guest_last()
 
     drain()
 
@@ -604,11 +703,14 @@
             pltpu.VMEM((block, block), BF16),
             pltpu.VMEM((block, block), BF16),
             pltpu.VMEM((block, block), F32),
+            pltpu.VMEM((n_pcol, depth, LANES), kind),
             dma((4,)),
             dma((n_pcol // 2, n_pieces - 1)),
             dma((n_pieces - 1,)),
             dma((n_pcol // 2,)),
             dma((6,)),
+            dma((5,)),
+            pltpu.SemaphoreType.REGULAR((2,)),
             dma((2,)),
             dma((chips - 1,)),
             dma((chips - 1,)),

time: 25.1 us -> 24.8 us (0.988)
  the two profiles are of different devices: /device:TPU:4 before, /device:TPU:0 now
where the time goes in v5:
time: 24.8 us; the launch traced here: 24.6 us
  Pallas kernels  24.6 us (99%)
    pallas_call x1, Pallas kernels, per_device(): pl.pallas_call(functools.partial(kernel, n_prow, n_pcol), out_shape=kept,...  23.3 us
    pallas_call x1, Pallas kernels, per_device(): pl.pallas_call(finish, out_shape=pltpu.HBM((rows, width), BF16), in_specs...  1.31 us

profile of v5, /device:TPU:0, one launch (start us, length us, event | category | flops | bytes accessed | tf_op | source)
XLA Modules:
  0.0 24.6 jit_solution(8257948259793088321)
XLA Ops:
  0.0 23.3 %shard_map.46 = (bf16[2048,384]{1,0:T(8,128)(2,1)S(1)}, bf16[8,64,2048]{2,1,0:T(8,128)(2,1)S(1)}, bf16[512,384]{1,0:T(8,128)(2,1)S(1)}, f32[256,384]{1,0:T(8,128)S(1)}, bf16[2048,384]{1,0:T(8,128)(2,1)S(1)}) custom-call(bf16[2048,384]{1,0:T(8,128)(2,1)} %slab_hbm.1, s32[1,512]{1,0:T(1,128)} %bitcast.1, bf16[512,512]{1,0:T(8,128)(2,1)} %l_top_hbm.1, ...), custom_call_target="tpu_custom_call" | custom-call | tf_op jit(solution)/shard_map/pallas_call | solution.py:690
  23.3 1.3 %shard_map.47 = bf16[2048,384]{1,0:T(8,128)(2,1)} custom-call(bf16[2048,384]{1,0:T(8,128)(2,1)S(1)} %get-tuple-element.10.done_ref, bf16[8,64,2048]{2,1,0:T(8,128)(2,1)S(1)} %get-tuple-element.11.gathered, bf16[512,384]{1,0:T(8,128)(2,1)S(1)} %get-tuple-element.12.u_ref, f32[256,384]{1,0:T(8,128)S(1)} %get-tuple-element.13.partial, ...), custom_call_target="tpu_custom_call" | custom-call | tf_op jit(solution)/shard_map/pallas_call | solution.py:722

commit v6 on v5

--- a/solution.py
+++ b/solution.py
@@ -180,8 +180,14 @@
     def neighbour(way):
         return me_c + 2 - 4 * way
 
+    def slot(at, level):
+        return at - (at > level).astype(jnp.int32)
+
     def line(way, at, piece, thick):
-        send(at * 2 + x, columns_of(piece, thick), sent.at[way if piece < 2 else 2 + way], line_recv.at[at, piece], neighbour(way))
+        send(
+            at * 2 + x, columns_of(piece, thick), sent.at[way if piece < 2 else 2 + way], line_recv.at[slot(at, z + 1 - 2 * way), piece],
+            neighbour(way),
+        )
 
     def cross(at, piece, thick):
         send(at * 2 + x, columns_of(piece, thick), sent.at[4], cross_recv.at[piece], z * 2 + other)
@@ -290,7 +296,7 @@
                 both_ways(lambda way: line(way, z, piece, thick))
                 cross(z, piece, thick)
             needed(piece, lambda: classed(z, piece, own))
-            if piece == 0:
+            if piece == 2:
                 by_class(z, lambda thick: send(
                     me_c, columns_of(rest, thick), sent.at[5], rest_recv.at[z], z * 2 + other
                 ))
@@ -330,7 +336,7 @@
                 (1, z + distance, z < length - distance, z > 0),
             ):
                 def pass_on(thick):
-                    landed(columns_of(piece, thick)[1], line_recv.at[at, piece])
+                    landed(columns_of(piece, thick)[1], line_recv.at[slot(at, z), piece])
                     pl.when(onward)(lambda: line(way, at, piece, thick))
                     cross(at, piece, thick)
 
@@ -629,16 +635,21 @@
     for act in plan:
         act()
 
+    def near_levels():
+        for distance in range(1, length - 1):
+            last_rests(distance)
+        start, size = columns_of(rest, False)
+        total = pivoted[start:start + size, :].astype(F32)
+        last = last_level(length)
+        for step in range(1, length):
+            total = total - level_of(gathered, u_ref, (last + step) % length, (start, size))
+        partial[...] = total
+
     for piece in bulk:
         if piece == 0:
-            for distance in range(1, length - 1):
-                last_rests(distance)
-            start, size = columns_of(rest, False)
-            total = pivoted[start:start + size, :].astype(F32)
-            last = last_level(length)
-            for step in range(1, length):
-                total = total - level_of(gathered, u_ref, (last + step) % length, (start, size))
-            partial[...] = total
+            pl.when(jnp.logical_not(lead))(near_levels)
+        if piece == tail - 1:
+            pl.when(lead)(near_levels)
         crossed(piece)
         if piece < tail:
             update(piece)
@@ -705,7 +716,7 @@
             pltpu.VMEM((block, block), F32),
             pltpu.VMEM((n_pcol, depth, LANES), kind),
             dma((4,)),
-            dma((n_pcol // 2, n_pieces - 1)),
+            dma((n_pcol // 2 - 1, n_pieces - 1)),
             dma((n_pieces - 1,)),
             dma((n_pcol // 2,)),
             dma((6,)),

time: 24.8 us -> 24.7 us (level)
  no operation moved by 1% of the time
where the time goes in v6:
time: 24.7 us; the launch traced here: 24.6 us
  Pallas kernels  24.6 us (100%)
    pallas_call x1, Pallas kernels, per_device(): pl.pallas_call(functools.partial(kernel, n_prow, n_pcol), out_shape=kept,...  23.2 us
    pallas_call x1, Pallas kernels, per_device(): pl.pallas_call(finish, out_shape=pltpu.HBM((rows, width), BF16), in_specs...  1.31 us

profile of v6, /device:TPU:0, one launch (start us, length us, event | category | flops | bytes accessed | tf_op | source)
XLA Modules:
  0.0 24.6 jit_solution(157327222199078040)
XLA Ops:
  0.0 23.2 %shard_map.46 = (bf16[2048,384]{1,0:T(8,128)(2,1)S(1)}, bf16[8,64,2048]{2,1,0:T(8,128)(2,1)S(1)}, bf16[512,384]{1,0:T(8,128)(2,1)S(1)}, f32[256,384]{1,0:T(8,128)S(1)}, bf16[2048,384]{1,0:T(8,128)(2,1)S(1)}) custom-call(bf16[2048,384]{1,0:T(8,128)(2,1)} %slab_hbm.1, s32[1,512]{1,0:T(1,128)} %bitcast.1, bf16[512,512]{1,0:T(8,128)(2,1)} %l_top_hbm.1, ...), custom_call_target="tpu_custom_call" | custom-call | tf_op jit(solution)/shard_map/pallas_call | solution.py:701
  23.3 1.3 %shard_map.47 = bf16[2048,384]{1,0:T(8,128)(2,1)} custom-call(bf16[2048,384]{1,0:T(8,128)(2,1)S(1)} %get-tuple-element.10.done_ref, bf16[8,64,2048]{2,1,0:T(8,128)(2,1)S(1)} %get-tuple-element.11.gathered, bf16[512,384]{1,0:T(8,128)(2,1)S(1)} %get-tuple-element.12.u_ref, f32[256,384]{1,0:T(8,128)S(1)} %get-tuple-element.13.partial, ...), custom_call_target="tpu_custom_call" | custom-call | tf_op jit(solution)/shard_map/pallas_call | solution.py:733

commit v7 on v6

--- a/solution.py
+++ b/solution.py
@@ -670,12 +670,12 @@
         return copy
 
     copies = [store(done_ref.at[pl.ds(0, edge)], 0, edge, 0)]
+    last = last_level(gathered.shape[0] // 2)
+    result[start - edge:, :] = (partial[...] - level_of(gathered, u_ref, last, (start, size))).astype(BF16)
+    copies.append(store(result.at[pl.ds(start - edge, size)], start, size, 1))
     panel = gathered[:, :, edge:start].reshape(block, start - edge).astype(BF16)
     result[:start - edge, :] = trailing(panel, u_ref[...], pivoted[edge:start, :])
     copies.append(store(result.at[pl.ds(0, start - edge)], edge, start - edge, 2))
-    last = last_level(gathered.shape[0] // 2)
-    result[start - edge:, :] = (partial[...] - level_of(gathered, u_ref, last, (start, size))).astype(BF16)
-    copies.append(store(result.at[pl.ds(start - edge, size)], start, size, 1))
     for copy in copies:
         copy.wait()
 

time: 24.7 us -> 24.7 us (level)
  no operation moved by 1% of the time
where the time goes in v7:
time: 24.7 us; the launch traced here: 24.6 us
  Pallas kernels  24.6 us (100%)
    pallas_call x1, Pallas kernels, per_device(): pl.pallas_call(functools.partial(kernel, n_prow, n_pcol), out_shape=kept,...  23.2 us
    pallas_call x1, Pallas kernels, per_device(): pl.pallas_call(finish, out_shape=pltpu.HBM((rows, width), BF16), in_specs...  1.33 us

profile of v7, /device:TPU:0, one launch (start us, length us, event | category | flops | bytes accessed | tf_op | source)
XLA Modules:
  0.0 24.6 jit_solution(18256234301628455564)
XLA Ops:
  0.0 23.2 %shard_map.46 = (bf16[2048,384]{1,0:T(8,128)(2,1)S(1)}, bf16[8,64,2048]{2,1,0:T(8,128)(2,1)S(1)}, bf16[512,384]{1,0:T(8,128)(2,1)S(1)}, f32[256,384]{1,0:T(8,128)S(1)}, bf16[2048,384]{1,0:T(8,128)(2,1)S(1)}) custom-call(bf16[2048,384]{1,0:T(8,128)(2,1)} %slab_hbm.1, s32[1,512]{1,0:T(1,128)} %bitcast.1, bf16[512,512]{1,0:T(8,128)(2,1)} %l_top_hbm.1, ...), custom_call_target="tpu_custom_call" | custom-call | tf_op jit(solution)/shard_map/pallas_call | solution.py:701
  23.3 1.3 %shard_map.47 = bf16[2048,384]{1,0:T(8,128)(2,1)} custom-call(bf16[2048,384]{1,0:T(8,128)(2,1)S(1)} %get-tuple-element.10.done_ref, bf16[8,64,2048]{2,1,0:T(8,128)(2,1)S(1)} %get-tuple-element.11.gathered, bf16[512,384]{1,0:T(8,128)(2,1)S(1)} %get-tuple-element.12.u_ref, f32[256,384]{1,0:T(8,128)S(1)} %get-tuple-element.13.partial, ...), custom_call_target="tpu_custom_call" | custom-call | tf_op jit(solution)/shard_map/pallas_call | solution.py:733
